TPU v7x, 32 devices: a whole 2x2x4 slice. The times are simulated.
32 devices in a mesh: grp: 2 (over x), aux: 16 (over z, y, core).
Axes of the slice: x: 2, y: 2, z: 4, core: 2. Of those that a mesh axis runs over, the one named last changes fastest.
Arguments:
- three_index: bfloat16 [64, 256, 256], P('aux'), may hold values from -0.375 to 0.375
- relaxed: bfloat16 [512, 256], P('grp'), parts along dimension 0, may hold values from -0.375 to 0.375
- plus_amplitude: bfloat16 [512, 256], P('grp'), parts along dimension 0, may hold values from -0.375 to 0.375
- minus_amplitude: bfloat16 [512, 256], P('grp'), parts along dimension 0, may hold values from -0.375 to 0.375
- ground: bfloat16 [256, 256], replicated, may hold values from -0.375 to 0.375
- integral_grad: bfloat16 [3, 64, 512, 256], P(None, None, 'aux'), may hold values from -0.09375 to 0.09375
- metric_grad: bfloat16 [3, 64, 64], P(None, 'aux'), may hold values from -0.5 to 0.5
- function_atom: int32 [256], replicated, may hold values from 0 to 31, never falling along the last dimension, each value on 1 to 16 neighbouring positions
- aux_center: int32 [64], P('aux'), may hold values from 0 to 31, never falling along the last dimension, each value on 1 to 4 neighbouring positions
- block_list: int32 [512], replicated, may hold values from 0 to 255, as said below
- block_count: int32 [16], replicated, may hold values from 0 to 32, as said below
Outputs:
- gradient: float32 [3, 64], P(None, 'grp'), parts along dimension 1
There are 2 independent parts, one for each index of `grp`. A program takes and returns all parts, laid end to end along the dimension named above; an argument that names none is the same for every part. Nothing has to cross between parts.
Inputs may be any that keep to these rules, and one draw needn't show every extreme that they name: block_count[d] is the number of live slots of owner d; the counts sum to 256, and at least one owner has 32. `block_list`: slot s of owner d is entry d * 32 + s and is live when s < block_count[d]; each tile pair i * 16 + j is held by exactly one live slot; slots that are not live hold arbitrary tile pairs.
All inputs are finite; a program needn't handle non-finite values.
Results may differ from a plain program's by a relative error of at most 0.0032.
Values may be sent and summed in bfloat16 or wider, within the bound.
No kernel may reach another device: no remote copies, remote signals or barrier semaphores. Data moves between devices by JAX's collectives and lax.ppermute only.
A program may use at most 64 MiB of HBM per device.

v0:
```python
import jax
import jax.numpy as jnp
from jax import lax
from jax.sharding import PartitionSpec as P

TILE = 16
NATOM = 32


def on_device(
    three_index,
    relaxed,
    plus_amplitude,
    minus_amplitude,
    ground,
    integral_grad,
    metric_grad,
    function_atom,
    aux_center,
    block_list,
    block_count,
):
    highest = lax.Precision.HIGHEST
    aux_local = three_index.shape[0]
    basis_count = three_index.shape[1]
    tile_count = basis_count // TILE
    slot_depth = integral_grad.shape[2]
    slot_total = block_list.shape[0]
    fitted = jnp.einsum("pab,ab->p", three_index, relaxed, preferred_element_type=jnp.float32)
    stacked = jnp.concatenate([plus_amplitude, minus_amplitude, ground], 0)
    halves = jnp.einsum(
        "ab,pbc->pac", stacked, three_index, preferred_element_type=jnp.float32
    ).astype(jnp.bfloat16)
    paired_half = halves[:, : 2 * basis_count].reshape(aux_local, 2, basis_count, basis_count)
    paired_half = jnp.concatenate([paired_half[:, 0], paired_half[:, 1]], axis=2)
    ground_half = halves[:, 2 * basis_count :]
    partners = jnp.concatenate([plus_amplitude, -minus_amplitude], axis=1)
    exchange_part = jnp.einsum(
        "pab,cb->pac", paired_half, partners, preferred_element_type=jnp.float32
    )
    crossed = jnp.einsum("pab,bc->pac", ground_half, relaxed, preferred_element_type=jnp.float32)
    triple = (
        fitted[:, None, None] * relaxed.astype(jnp.float32)[None]
        + exchange_part
        + crossed
        + jnp.swapaxes(crossed, 1, 2)
    )
    triple = triple.astype(jnp.bfloat16)
    blocked = triple.reshape(aux_local, tile_count, TILE, tile_count, TILE).transpose(0, 1, 3, 2, 4)
    blocked = blocked.reshape(aux_local, tile_count * tile_count, TILE * TILE)
    chosen = jnp.take(blocked, block_list, axis=1)
    slot_ids = jnp.arange(slot_total, dtype=jnp.int32)
    live_mask = (slot_ids % slot_depth < block_count[slot_ids // slot_depth]).astype(jnp.float32)
    arrived = lax.all_to_all(chosen, "aux", split_axis=1, concat_axis=0, tiled=True)
    first_slot = lax.axis_index("aux") * slot_depth
    tile_ids = lax.dynamic_slice_in_dim(block_list, first_slot, slot_depth)
    slot_mask = lax.dynamic_slice_in_dim(live_mask, first_slot, slot_depth)
    contracted = jnp.einsum(
        "pgf,kpgf->kgf", arrived, integral_grad, preferred_element_type=jnp.float32
    )
    slot_count = tile_ids.shape[0]
    row_sums = contracted.reshape(3, slot_count, TILE, TILE).sum(axis=3) * slot_mask[None, :, None]
    function_ids = (tile_ids // tile_count)[:, None] * TILE + jnp.arange(TILE, dtype=jnp.int32)[
        None, :
    ]
    atom_table = (
        function_atom[function_ids][:, :, None] == jnp.arange(NATOM, dtype=jnp.int32)[None, None, :]
    ).astype(jnp.float32)
    three_part = 2.0 * jnp.einsum("kgm,gma->ka", row_sums, atom_table, precision=highest)
    all_fitted = lax.all_gather(fitted, "aux", axis=0, tiled=True)
    coupling = jnp.einsum(
        "kpq,q->kp", metric_grad.astype(jnp.float32), all_fitted, precision=highest
    )
    aux_table = (aux_center[:, None] == jnp.arange(NATOM, dtype=jnp.int32)[None, :]).astype(
        jnp.float32
    )
    metric_part = jnp.einsum("kp,pa->ka", coupling * fitted[None, :], aux_table, precision=highest)
    return lax.psum(three_part - metric_part, "aux")


def solution(mesh):
    in_specs = (
        P("aux", None, None),
        P("grp", None),
        P("grp", None),
        P("grp", None),
        P(),
        P(None, None, "aux", None),
        P(None, "aux", None),
        P(),
        P("aux"),
        P(),
        P(),
    )
    out_specs = P(None, "grp")
    return jax.shard_map(
        on_device, mesh=mesh, in_specs=in_specs, out_specs=out_specs, check_vma=False
    )
```

profile of v0, /device:TPU:0, one launch (start us, length us, event | category | flops | bytes accessed | tf_op | source)
XLA Modules:
  0.0 119.7 jit_solution(17670021363365028496)
XLA Ops:
  0.0 1.8 %fusion = bf16[4,768,256]{2,1,0:T(8,128)(2,1)S(1)} fusion(bf16[4,256,256]{2,1,0:T(8,128)(2,1)} %param.11, bf16[256,256]{1,0:T(8,128)(2,1)} %param.15, bf16[256,256]{1,0:T(8,128)(2,1)} %param.14, bf16[256,256]{1,0:T(8,128)(2,1)} %param.13), kind=kOutput, calls=%fused_computation.5 | convolution fusion | flops 404619264 | bytes 2490368 | tf_op jit(solution)/shard_map/ab,pbc->pac/dot_general | solution.py:31
  2.3 0.5 copy-done.6
  2.8 0.7 neg.3
  3.5 0.9 slice_bitcast_fusion.1
  4.3 0.3 copy.42
  4.7 1.9 %convolution_bitcast_fusion.1 = f32[4]{0:T(128)S(1)} fusion(bf16[4,256,256]{2,1,0:T(8,128)(2,1)S(1)} %copy-done.4, bf16[256,256,1]{1,0,2:T(8,128)(2,1)} %bitcast.80), kind=kOutput, calls=%fused_computation.13 | convolution fusion | flops 524288 | bytes 655376 | tf_op jit(solution)/shard_map/pab,ab->p/dot_general | solution.py:29
  6.6 0.5 copy-done.11
  7.1 0.5 fusion.3
  7.6 4.2 %reshape.108 = bf16[4,16,16,16,16]{4,3,2,1,0:T(8,128)(2,1)} reshape(bf16[4,256,256]{2,1,0:T(8,128)(2,1)S(1)} %fusion.3) | data formatting | bytes 1048576 | tf_op jit(solution)/shard_map/reshape | solution.py:49
  11.7 5.2 %copy.74 = bf16[4,16,16,16,16]{4,2,3,1,0:T(8,128)(2,1)} copy(bf16[4,16,16,16,16]{4,3,2,1,0:T(8,128)(2,1)} %reshape.108) | data formatting | bytes 1048576 | tf_op jit(solution)/shard_map/reshape | solution.py:49
  17.0 5.5 %reshape.109 = bf16[4,256,256]{2,1,0:T(8,128)(2,1)S(1)} reshape(bf16[4,16,16,16,16]{4,3,2,1,0:T(8,128)(2,1)} %bitcast.77) | data formatting | bytes 1048576 | tf_op jit(solution)/shard_map/reshape | solution.py:50
  22.5 0.4 copy.44
  22.9 2.4 %gather_fusion = bf16[512,4,256]{2,1,0:T(4,128)(2,1)S(1)} fusion(bf16[4,256,256]{2,0,1:T(4,128)(2,1)S(1)} %copy.44, s32[1024]{0:T(1024)S(1)} %pad_clamp_fusion.1), kind=kCustom, calls=%fused_computation | custom fusion | bytes 2099200 | tf_op jit(solution)/shard_map/jit(_take)/gather | solution.py:51
  25.3 2.7 %select_bitcast_fusion = bf16[4,512,256]{2,0,1:T(4,128)(2,1)} fusion(bf16[512,4,256]{2,1,0:T(4,128)(2,1)S(1)} %gather_fusion, pred[512]{0:T(512)(128)(4,1)S(1)} %compare_and_fusion), kind=kLoop, calls=%fused_computation.18 | loop fusion | flops 524288 | bytes 2097664 | tf_op jit(solution)/shard_map/jit(_take)/select_n | solution.py:51
  28.0 7.4 %all-to-all-start = ((bf16[4,512,256]{2,0,1:T(4,128)(2,1)}), bf16[4,512,256]{2,0,1:T(4,128)(2,1)S(1)}, u32[]{:S(2)}, u32[]{:S(2)}) async-start(bf16[4,512,256]{2,0,1:T(4,128)(2,1)} %select_bitcast_fusion), calls=%async_computation | async-start | bytes 2097152 | tf_op jit(solution)/shard_map/all_to_all | solution.py:54
  35.7 0.7 fusion.34
  36.5 4.3 %compare_select_fusion.2 = s32[512,1]{0,1:T(1,128)S(1)} fusion(s32[]{:T(128)} %bitcast.30, s32[]{:T(128)} %bitcast.31, s32[]{:T(128)} %bitcast.32, s32[]{:T(128)} %bitcast.33, s32[]{:T(128)} %bitcast.34, s32[]{:T(128)} %bitcast.36, s32[]{:T(128)} %bitcast.35), kind=kLoop, calls=%fused_computation.49 | loop fusion | flops 11776 | bytes 2076 | tf_op jit(solution)/shard_map/gather | solution.py:53
  40.8 5.7 %fusion.25 = f32[512]{0:T(512)S(1)} fusion(pred[512]{0:T(512)(128)(4,1)S(1)} %compare_reduce_fusion, pred[512]{0:T(512)(128)(4,1)S(1)} %compare_reduce_fusion.1, pred[512]{0:T(512)(128)(4,1)S(1)} %compare_reduce_fusion.2, pred[512]{0:T(512)(128)(4,1)S(1)} %compare_reduce_fusion.3, pred[512]{0:T(512)(128)(4,1)S(1)} %compare_reduce_fusion.4, ...), kind=kLoop, calls=%fused_computation.73 | loop fusion | flops 8704 | bytes 8740 | tf_op jit(solution)/shard_map/convert_element_type | solution.py:53
  46.8 3.5 %gather_fusion.1 = s32[512]{0:T(512)S(1)} fusion(s32[256]{0:T(256)S(1)} %copy-done.1, s32[1024]{0:T(1024)S(1)} %pad_clamp_fusion), kind=kCustom, calls=%fused_computation.1 | custom fusion | bytes 6144 | tf_op jit(solution)/shard_map/gather | solution.py:67
  50.5 0.6 dynamic-slice
  52.0 33.9 %all-reduce = f32[64]{0:T(128)S(1)} all-reduce(f32[64]{0:T(128)S(1)} %dynamic-update-slice), channel_id=1, replica_groups=mesh['grp'=2,'aux'=16] {'aux'}, use_global_device_ids=true, to_apply=%add | all-reduce | flops 64 | bytes 512
  86.6 1.5 %copy-done.2 = bf16[3,64,32,256]{3,2,1,0:T(8,128)(2,1)S(1)} copy-done((bf16[3,64,32,256]{3,2,1,0:T(8,128)(2,1)S(1)}, bf16[3,64,32,256]{3,2,1,0:T(8,128)(2,1)}, u32[]{:S(2)}) %copy-start.2) | copy-done | bytes 3145752
  88.2 0.7 multiply_reduce_fusion
  89.7 30.1 %psum.7 = f32[3,32]{1,0:T(4,128)} all-reduce(f32[3,32]{1,0:T(4,128)S(1)} %convolution_subtract_fusion), channel_id=1, replica_groups=mesh['grp'=2,'aux'=16] {'aux'}, use_global_device_ids=true, to_apply=%region_1.2 | all-reduce | flops 96 | bytes 768 | tf_op jit(solution)/shard_map/psum | solution.py:78
  (60 shorter events, 2.9 us)
Async XLA Ops:
  0.0 85.9 %copy-start = (bf16[3,4,64]{2,1,0:T(4,128)(2,1)S(1)}, bf16[3,4,64]{2,1,0:T(4,128)(2,1)}, u32[]{:S(2)}) copy-start(bf16[3,4,64]{2,1,0:T(4,128)(2,1)} %param.17) | copy-start | bytes 4612
  0.0 2.0 %copy-start.8 = (bf16[256,256]{1,0:T(8,128)(2,1)S(1)}, bf16[256,256]{1,0:T(8,128)(2,1)}, u32[]{:S(2)}) copy-start(bf16[256,256]{1,0:T(8,128)(2,1)} %param.12) | copy-start | bytes 393220
  1.9 0.9 copy-start.6
  1.9 1.6 %copy-start.10 = (s32[512]{0:T(512)S(1)}, s32[512]{0:T(512)}, u32[]{:S(2)}) copy-start(s32[512]{0:T(512)} %param.20) | copy-start | bytes 6148
  3.5 1.2 %copy-start.4 = (bf16[4,256,256]{2,1,0:T(8,128)(2,1)S(1)}, bf16[4,256,256]{2,1,0:T(8,128)(2,1)}, u32[]{:S(2)}) copy-start(bf16[4,256,256]{2,1,0:T(8,128)(2,1)} %param.11) | copy-start | bytes 1572868
  4.3 2.8 %copy-start.5 = (bf16[256,256]{1,0:T(8,128)(2,1)S(1)}, bf16[256,256]{1,0:T(8,128)(2,1)}, u32[]{:S(2)}) copy-start(bf16[256,256]{1,0:T(8,128)(2,1)} %param.13) | copy-start | bytes 393220
  4.7 2.4 %copy-start.3 = (bf16[4,256,256]{2,1,0:T(8,128)(2,1)S(1)}, bf16[4,256,256]{2,1,0:T(8,128)(2,1)}, u32[]{:S(2)}) copy-start(bf16[4,256,256]{2,1,0:T(8,128)(2,1)} %get-tuple-element.6) | copy-start | bytes 1572868
  4.7 2.4 %copy-start.7 = (bf16[256,256]{1,0:T(8,128)(2,1)S(1)}, bf16[256,256]{1,0:T(8,128)(2,1)}, u32[]{:S(2)}) copy-start(bf16[256,256]{1,0:T(8,128)(2,1)} %neg.3) | copy-start | bytes 393220
  6.6 0.5 copy-start.11
  25.3 10.4 %copy-start.9 = (s32[16]{0:T(128)S(1)}, s32[16]{0:T(128)}, u32[]{:S(2)}) copy-start(s32[16]{0:T(128)} %param.21) | copy-start | bytes 196
  25.3 21.4 %copy-start.1 = (s32[256]{0:T(256)S(1)}, s32[256]{0:T(256)}, u32[]{:S(2)}) copy-start(s32[256]{0:T(256)} %param.18) | copy-start | bytes 3076
  28.0 58.0 %all-to-all-start = ((bf16[4,512,256]{2,0,1:T(4,128)(2,1)}), bf16[4,512,256]{2,0,1:T(4,128)(2,1)S(1)}, u32[]{:S(2)}, u32[]{:S(2)}) async-start(bf16[4,512,256]{2,0,1:T(4,128)(2,1)} %select_bitcast_fusion), calls=%async_computation | async-start | bytes 2097152 | tf_op jit(solution)/shard_map/all_to_all | solution.py:54
  46.8 3.7 %copy-start.14 = (u32[32]{0:T(128)S(1)}, u32[32]{0:T(128)}, u32[]{:S(2)}) copy-start(u32[32]{0:T(128)} %constant.97) | copy-start | bytes 388
  46.8 4.9 %copy-start.12 = (f32[4]{0:T(128)S(1)}, f32[4]{0:T(128)}, u32[]{:S(2)}) copy-start(f32[4]{0:T(128)} %copy-done.11) | copy-start | bytes 52
  86.3 1.9 %copy-start.2 = (bf16[3,64,32,256]{3,2,1,0:T(8,128)(2,1)S(1)}, bf16[3,64,32,256]{3,2,1,0:T(8,128)(2,1)}, u32[]{:S(2)}) copy-start(bf16[3,64,32,256]{3,2,1,0:T(8,128)(2,1)} %param.16) | copy-start | bytes 9437188
  88.2 1.3 %copy-start.13 = (s32[4]{0:T(128)S(1)}, s32[4]{0:T(128)}, u32[]{:S(2)}) copy-start(s32[4]{0:T(128)} %param.19) | copy-start | bytes 52
where the time goes:
time: 120 us
  blocking collectives  64 us (53%)
  local copies, waits for them, and re-layouts  27.3 us (23%)
  other arithmetic  15 us (12%)
  starting transfers between devices  7.41 us (6%)
  matrix products  5.13 us (4%)
    unnamed x1, blocking collectives  33.9 us
    psum x1, blocking collectives, on_device(): return lax.psum(three_part - metric_part, 'aux')  30.1 us
    reshape x2, local copies, waits for them, and re-layouts, on_device(): triple.reshape(aux_local, tile_count, TILE, tile_count, TILE)  9.39 us
    all_to_all x1, starting transfers between devices, on_device(): lax.all_to_all(chosen, 'aux', split_axis=1, concat_axis=0, tiled=True)  7.41 us
    reshape x2, local copies, waits for them, and re-layouts, on_device(): blocked = blocked.reshape(aux_local, tile_count * tile_count, TILE * TILE)  5.89 us
    convert_element_type x1, other arithmetic, on_device(): (slot_ids % slot_depth < block_count[slot_ids // slot_depth]).astype(jnp....  5.67 us
    gather x10, other arithmetic, on_device(): block_count[slot_ids // slot_depth]  4.61 us
    gather x3, local copies, waits for them, and re-layouts, on_device(): function_atom[function_ids][:, :, None]  3.67 us
  transfers between devices with their start and end apart: 1, of which 0 were waited for; matrix products, arithmetic and copies ran while one was open for 13% of the time, Pallas kernels for 0%

commit v1 on v0

--- a/solution.py
+++ b/solution.py
@@ -75,7 +75,7 @@
         jnp.float32
     )
     metric_part = jnp.einsum("kp,pa->ka", coupling * fitted[None, :], aux_table, precision=highest)
-    return lax.psum(three_part - metric_part, "aux")
+    return jnp.sum(lax.all_gather(three_part - metric_part, "aux"), axis=0)
 
 
 def solution(mesh):

time: 120 us -> 108 us (0.900)
  blocking collectives: 64 us -> 51.1 us
    psum x1 -> x0, blocking collectives: 30.1 us -> none  [on_device(): return lax.psum(three_part - metric_part, 'aux')]
    all_gather x0 -> x1, blocking collectives: none -> 17.2 us  [on_device(): return jnp.sum(lax.all_gather(three_part - metric_part, 'aux'), axis=0)]
  transfers between devices with their start and end apart: 1 -> 1, of which waited for: 0 -> 0; matrix products, arithmetic and copies ran while one was open for 13% -> 15% of each run, Pallas kernels for 0% -> 0%
where the time goes in v1:
time: 108 us; the launch traced here: 107 us
  blocking collectives  51.1 us (47%)
  local copies, waits for them, and re-layouts  27.3 us (25%)
  other arithmetic  15.6 us (14%)
  starting transfers between devices  7.41 us (7%)
  matrix products  5.13 us (5%)
    unnamed x1, blocking collectives  33.9 us
    all_gather x1, blocking collectives, on_device(): return jnp.sum(lax.all_gather(three_part - metric_part, 'aux'), axis=0)  17.2 us
    reshape x2, local copies, waits for them, and re-layouts, on_device(): triple.reshape(aux_local, tile_count, TILE, tile_count, TILE)  9.39 us
    all_to_all x1, starting transfers between devices, on_device(): lax.all_to_all(chosen, 'aux', split_axis=1, concat_axis=0, tiled=True)  7.41 us
    reshape x2, local copies, waits for them, and re-layouts, on_device(): blocked = blocked.reshape(aux_local, tile_count * tile_count, TILE * TILE)  5.89 us
    convert_element_type x1, other arithmetic, on_device(): (slot_ids % slot_depth < block_count[slot_ids // slot_depth]).astype(jnp....  5.67 us
    gather x10, other arithmetic, on_device(): block_count[slot_ids // slot_depth]  4.61 us
    gather x3, local copies, waits for them, and re-layouts, on_device(): function_atom[function_ids][:, :, None]  3.67 us
  transfers between devices with their start and end apart: 1, of which 0 were waited for; matrix products, arithmetic and copies ran while one was open for 15% of the time, Pallas kernels for 0%

profile of v1, /device:TPU:0, one launch (start us, length us, event | category | flops | bytes accessed | tf_op | source)
XLA Modules:
  0.0 107.5 jit_solution(15786463537390900283)
XLA Ops:
  0.0 1.8 %fusion = bf16[4,768,256]{2,1,0:T(8,128)(2,1)S(1)} fusion(bf16[4,256,256]{2,1,0:T(8,128)(2,1)} %param.11, bf16[256,256]{1,0:T(8,128)(2,1)} %param.15, bf16[256,256]{1,0:T(8,128)(2,1)} %param.14, bf16[256,256]{1,0:T(8,128)(2,1)} %param.13), kind=kOutput, calls=%fused_computation.5 | convolution fusion | flops 404619264 | bytes 2490368 | tf_op jit(solution)/shard_map/ab,pbc->pac/dot_general | solution.py:31
  2.3 0.5 copy-done.6
  2.8 0.7 neg.3
  3.5 0.9 slice_bitcast_fusion.1
  4.7 1.9 %convolution_bitcast_fusion.1 = f32[4]{0:T(128)S(1)} fusion(bf16[4,256,256]{2,1,0:T(8,128)(2,1)S(1)} %copy-done.4, bf16[256,256,1]{1,0,2:T(8,128)(2,1)} %bitcast.82), kind=kOutput, calls=%fused_computation.14 | convolution fusion | flops 524288 | bytes 655376 | tf_op jit(solution)/shard_map/pab,ab->p/dot_general | solution.py:29
  6.6 0.5 copy-done.11
  7.1 0.5 fusion.3
  7.6 4.2 %reshape.108 = bf16[4,16,16,16,16]{4,3,2,1,0:T(8,128)(2,1)} reshape(bf16[4,256,256]{2,1,0:T(8,128)(2,1)S(1)} %fusion.3) | data formatting | bytes 1048576 | tf_op jit(solution)/shard_map/reshape | solution.py:49
  11.7 5.2 %copy.81 = bf16[4,16,16,16,16]{4,2,3,1,0:T(8,128)(2,1)} copy(bf16[4,16,16,16,16]{4,3,2,1,0:T(8,128)(2,1)} %reshape.108) | data formatting | bytes 1048576 | tf_op jit(solution)/shard_map/reshape | solution.py:49
  17.0 5.5 %reshape.109 = bf16[4,256,256]{2,1,0:T(8,128)(2,1)S(1)} reshape(bf16[4,16,16,16,16]{4,3,2,1,0:T(8,128)(2,1)} %bitcast.79) | data formatting | bytes 1048576 | tf_op jit(solution)/shard_map/reshape | solution.py:50
  22.5 0.4 copy.51
  22.9 2.4 %gather_fusion = bf16[512,4,256]{2,1,0:T(4,128)(2,1)S(1)} fusion(bf16[4,256,256]{2,0,1:T(4,128)(2,1)S(1)} %copy.51, s32[1024]{0:T(1024)S(1)} %pad_clamp_fusion.1), kind=kCustom, calls=%fused_computation | custom fusion | bytes 2099200 | tf_op jit(solution)/shard_map/jit(_take)/gather | solution.py:51
  25.3 2.7 %select_bitcast_fusion = bf16[4,512,256]{2,0,1:T(4,128)(2,1)} fusion(bf16[512,4,256]{2,1,0:T(4,128)(2,1)S(1)} %gather_fusion, pred[512]{0:T(512)(128)(4,1)S(1)} %compare_and_fusion), kind=kLoop, calls=%fused_computation.19 | loop fusion | flops 524288 | bytes 2097664 | tf_op jit(solution)/shard_map/jit(_take)/select_n | solution.py:51
  28.0 7.4 %all-to-all-start = ((bf16[4,512,256]{2,0,1:T(4,128)(2,1)}), bf16[4,512,256]{2,0,1:T(4,128)(2,1)S(1)}, u32[]{:S(2)}, u32[]{:S(2)}) async-start(bf16[4,512,256]{2,0,1:T(4,128)(2,1)} %select_bitcast_fusion), calls=%async_computation | async-start | bytes 2097152 | tf_op jit(solution)/shard_map/all_to_all | solution.py:54
  35.7 0.7 fusion.35
  36.5 4.3 %compare_select_fusion.2 = s32[512,1]{0,1:T(1,128)S(1)} fusion(s32[]{:T(128)} %bitcast.30, s32[]{:T(128)} %bitcast.31, s32[]{:T(128)} %bitcast.32, s32[]{:T(128)} %bitcast.33, s32[]{:T(128)} %bitcast.34, s32[]{:T(128)} %bitcast.36, s32[]{:T(128)} %bitcast.35), kind=kLoop, calls=%fused_computation.50 | loop fusion | flops 11776 | bytes 2076 | tf_op jit(solution)/shard_map/gather | solution.py:53
  40.8 5.7 %fusion.26 = f32[512]{0:T(512)S(1)} fusion(pred[512]{0:T(512)(128)(4,1)S(1)} %compare_reduce_fusion, pred[512]{0:T(512)(128)(4,1)S(1)} %compare_reduce_fusion.1, pred[512]{0:T(512)(128)(4,1)S(1)} %compare_reduce_fusion.2, pred[512]{0:T(512)(128)(4,1)S(1)} %compare_reduce_fusion.3, pred[512]{0:T(512)(128)(4,1)S(1)} %compare_reduce_fusion.4, ...), kind=kLoop, calls=%fused_computation.74 | loop fusion | flops 8704 | bytes 8740 | tf_op jit(solution)/shard_map/convert_element_type | solution.py:53
  46.8 3.5 %gather_fusion.1 = s32[512]{0:T(512)S(1)} fusion(s32[256]{0:T(256)S(1)} %copy-done.1, s32[1024]{0:T(1024)S(1)} %pad_clamp_fusion), kind=kCustom, calls=%fused_computation.1 | custom fusion | bytes 6144 | tf_op jit(solution)/shard_map/gather | solution.py:67
  50.5 0.6 dynamic-slice
  52.0 33.9 %all-reduce = f32[64]{0:T(128)S(1)} all-reduce(f32[64]{0:T(128)S(1)} %dynamic-update-slice), channel_id=1, replica_groups=mesh['grp'=2,'aux'=16] {'aux'}, use_global_device_ids=true, to_apply=%add | all-reduce | flops 64 | bytes 512
  86.6 1.5 %copy-done.2 = bf16[3,64,32,256]{3,2,1,0:T(8,128)(2,1)S(1)} copy-done((bf16[3,64,32,256]{3,2,1,0:T(8,128)(2,1)S(1)}, bf16[3,64,32,256]{3,2,1,0:T(8,128)(2,1)}, u32[]{:S(2)}) %copy-start.2) | copy-done | bytes 3145752
  88.2 0.7 multiply_reduce_fusion
  89.7 17.2 %all-gather.1 = f32[16,3,32]{2,1,0:T(4,128)S(1)} all-gather(f32[1,3,32]{2,1,0:T(4,128)S(1)} %fusion.4), channel_id=2, replica_groups=mesh['grp'=2,'aux'=16] {'aux'}, dimensions={0}, use_global_device_ids=true | all-gather | bytes 6528 | tf_op jit(solution)/shard_map/all_gather | solution.py:78
  106.9 0.6 reduce_sum.19
  (61 shorter events, 3.2 us)
Async XLA Ops:
  0.0 85.9 %copy-start = (bf16[3,4,64]{2,1,0:T(4,128)(2,1)S(1)}, bf16[3,4,64]{2,1,0:T(4,128)(2,1)}, u32[]{:S(2)}) copy-start(bf16[3,4,64]{2,1,0:T(4,128)(2,1)} %param.17) | copy-start | bytes 4612
  0.0 2.0 %copy-start.8 = (bf16[256,256]{1,0:T(8,128)(2,1)S(1)}, bf16[256,256]{1,0:T(8,128)(2,1)}, u32[]{:S(2)}) copy-start(bf16[256,256]{1,0:T(8,128)(2,1)} %param.12) | copy-start | bytes 393220
  1.9 0.9 copy-start.6
  1.9 1.6 %copy-start.10 = (s32[512]{0:T(512)S(1)}, s32[512]{0:T(512)}, u32[]{:S(2)}) copy-start(s32[512]{0:T(512)} %param.20) | copy-start | bytes 6148
  3.5 1.2 %copy-start.4 = (bf16[4,256,256]{2,1,0:T(8,128)(2,1)S(1)}, bf16[4,256,256]{2,1,0:T(8,128)(2,1)}, u32[]{:S(2)}) copy-start(bf16[4,256,256]{2,1,0:T(8,128)(2,1)} %param.11) | copy-start | bytes 1572868
  4.3 2.8 %copy-start.5 = (bf16[256,256]{1,0:T(8,128)(2,1)S(1)}, bf16[256,256]{1,0:T(8,128)(2,1)}, u32[]{:S(2)}) copy-start(bf16[256,256]{1,0:T(8,128)(2,1)} %param.13) | copy-start | bytes 393220
  4.7 2.4 %copy-start.3 = (bf16[4,256,256]{2,1,0:T(8,128)(2,1)S(1)}, bf16[4,256,256]{2,1,0:T(8,128)(2,1)}, u32[]{:S(2)}) copy-start(bf16[4,256,256]{2,1,0:T(8,128)(2,1)} %get-tuple-element.6) | copy-start | bytes 1572868
  4.7 2.4 %copy-start.7 = (bf16[256,256]{1,0:T(8,128)(2,1)S(1)}, bf16[256,256]{1,0:T(8,128)(2,1)}, u32[]{:S(2)}) copy-start(bf16[256,256]{1,0:T(8,128)(2,1)} %neg.3) | copy-start | bytes 393220
  6.6 0.5 copy-start.11
  25.3 10.4 %copy-start.9 = (s32[16]{0:T(128)S(1)}, s32[16]{0:T(128)}, u32[]{:S(2)}) copy-start(s32[16]{0:T(128)} %param.21) | copy-start | bytes 196
  25.3 21.4 %copy-start.1 = (s32[256]{0:T(256)S(1)}, s32[256]{0:T(256)}, u32[]{:S(2)}) copy-start(s32[256]{0:T(256)} %param.18) | copy-start | bytes 3076
  28.0 58.0 %all-to-all-start = ((bf16[4,512,256]{2,0,1:T(4,128)(2,1)}), bf16[4,512,256]{2,0,1:T(4,128)(2,1)S(1)}, u32[]{:S(2)}, u32[]{:S(2)}) async-start(bf16[4,512,256]{2,0,1:T(4,128)(2,1)} %select_bitcast_fusion), calls=%async_computation | async-start | bytes 2097152 | tf_op jit(solution)/shard_map/all_to_all | solution.py:54
  46.8 3.7 %copy-start.14 = (u32[32]{0:T(128)S(1)}, u32[32]{0:T(128)}, u32[]{:S(2)}) copy-start(u32[32]{0:T(128)} %constant.97) | copy-start | bytes 388
  46.8 4.9 %copy-start.12 = (f32[4]{0:T(128)S(1)}, f32[4]{0:T(128)}, u32[]{:S(2)}) copy-start(f32[4]{0:T(128)} %copy-done.11) | copy-start | bytes 52
  86.3 1.9 %copy-start.2 = (bf16[3,64,32,256]{3,2,1,0:T(8,128)(2,1)S(1)}, bf16[3,64,32,256]{3,2,1,0:T(8,128)(2,1)}, u32[]{:S(2)}) copy-start(bf16[3,64,32,256]{3,2,1,0:T(8,128)(2,1)} %param.16) | copy-start | bytes 9437188
  88.2 1.3 %copy-start.13 = (s32[4]{0:T(128)S(1)}, s32[4]{0:T(128)}, u32[]{:S(2)}) copy-start(s32[4]{0:T(128)} %param.19) | copy-start | bytes 52
